TPU v7x, 32 devices: a whole 2x2x4 slice. The times are simulated.
32 devices in a mesh: row: 8 (over z, x), col: 4 (over y, core).
Axes of the slice: x: 2, y: 2, z: 4, core: 2. Of those that a mesh axis runs over, the one named last changes fastest.
Arguments:
- prior_scores: float32 [12288, 12288], P('row', 'col'), may hold values from 0.001 to 10
- tiles_first: bfloat16 [96, 5, 128, 128], P('row'), may hold values from 0 to 1, as said below
- columns_first: int32 [96, 5], P('row'), may hold values from 0 to 95, as said below
- tiles_second: bfloat16 [96, 5, 128, 128], P('col'), may hold values from 0 to 1, as said below
- columns_second: int32 [96, 5], P('col'), may hold values from 0 to 95, as said below
Outputs:
- alignment: float32 [12288, 12288], P('row', 'col')
Inputs may be any that keep to these rules, and one draw needn't show every extreme that they name: `tiles_first`: in every block row, the block in the first slot has entries of 0.5 or more on its diagonal. `tiles_second`: in every block row, the block in the first slot has entries of 0.5 or more on its diagonal. `columns_first`: each block row lists 5 different block columns. `columns_second`: each block row lists 5 different block columns.
All inputs are finite; a program needn't handle non-finite values.
Results may differ from a plain program's by a relative error of at most 0.0004.
The roundings to bfloat16 on the way count: a program that leaves them out, or rounds other values in their place, can miss the bound.
Values may be sent and summed in bfloat16 or wider, within the bound.
A program may use at most 192 MiB of HBM per device.

v0:
```python
import jax
import jax.numpy as jnp
from jax import lax
from jax.sharding import PartitionSpec as P

ITERS = 2
mixing = 0.8


def second_product(features, tile_set, columns, inverse):
    tile_size = tile_set.shape[2]
    blocks = features.reshape(-1, tile_size, features.shape[1])
    picked = jnp.take(blocks, columns, axis=0)
    result = jnp.einsum("jsoi,jsin->jon", tile_set, picked, preferred_element_type=jnp.float32)
    result = result.reshape(-1, features.shape[1]) * inverse[:, None]
    return result.astype(jnp.bfloat16)


def first_product(slab_data, tile_set, columns, inverse):
    tile_size = tile_set.shape[2]
    blocks = slab_data.reshape(slab_data.shape[0], -1, tile_size)
    picked = jnp.take(blocks, columns, axis=1)
    result = jnp.einsum("cisk,isok->cio", picked, tile_set, preferred_element_type=jnp.float32)
    result = result.reshape(slab_data.shape[0], -1) * inverse[None, :]
    return result.astype(jnp.bfloat16)


def local(prior_scores, tiles_first, columns_first, tiles_second, columns_second):
    prior_cols = prior_scores.T
    row_count = lax.axis_size("row")
    cell_count = float(
        prior_scores.shape[0] * row_count * prior_scores.shape[1] * lax.axis_size("col")
    )
    all_first, all_columns = (
        lax.all_gather(tiles_first, "row", axis=0, tiled=True),
        lax.all_gather(columns_first, "row", axis=0, tiled=True),
    )
    inverse_first = 1.0 / jnp.sum(all_first, axis=(1, 3), dtype=jnp.float32).reshape(-1)
    inverse_second = 1.0 / jnp.sum(tiles_second, axis=(1, 3), dtype=jnp.float32).reshape(-1)
    prior_sum = lax.psum(jnp.sum(prior_cols), ("row", "col"))
    current_state = prior_cols
    for iteration in range(ITERS):
        current = current_state.astype(jnp.bfloat16)
        gathered = lax.all_gather(current, "col", axis=0, tiled=True)
        mixed_cols = second_product(gathered, tiles_second, columns_second, inverse_second)
        slab_data = lax.all_to_all(mixed_cols, "row", split_axis=0, concat_axis=1, tiled=True)
        propagated = first_product(slab_data, all_first, all_columns, inverse_first)
        partial_value = jnp.sum(propagated.astype(jnp.float32))
        returned = lax.all_to_all(propagated, "row", split_axis=1, concat_axis=0, tiled=True)
        slab_sum = lax.psum(partial_value, ("row", "col"))
        grand_total = mixing * slab_sum + (1.0 - mixing) * prior_sum
        updated = mixing * returned.astype(jnp.float32) + (1.0 - mixing) * prior_cols
        current_state = updated / (grand_total / cell_count)
    return current_state.T


def solution(mesh):
    return jax.shard_map(
        local,
        mesh=mesh,
        in_specs=(
            P("row", "col"),
            P("row", None, None, None),
            P("row", None),
            P("col", None, None, None),
            P("col", None),
        ),
        out_specs=P("row", "col"),
        check_vma=False,
    )
```

profile of v0, /device:TPU:0, one launch (start us, length us, event | category | flops | bytes accessed | tf_op | source)
XLA Modules:
  0.0 1965.2 jit_solution(3482156097374935337)
XLA Ops:
  6.5 20.0 %fusion.28 = (f32[]{:T(128)}, bf16[3072,1536]{0,1:T(8,128)(2,1)}) fusion(f32[1536,3072]{1,0:T(8,128)} %param.9), kind=kLoop, calls=%fused_computation.55 | loop fusion | flops 9437183 | bytes 28311556 | tf_op jit(solution)/shard_map/reduce_sum | solution.py:40
  26.5 0.0 all-gather.5.cloned.1.call-update
  26.6 0.0 all-gather.7.cloned.1.call-start
  26.6 0.7 all-gather.7.cloned.1.call-update
  27.3 0.1 copy.33
  27.5 0.1 copy.37
  27.5 0.1 reshape.154
  27.6 2.7 convert_reduce_fusion.3
  30.4 226.2 %all-gather.5.cloned.1.call-done = bf16[12288,1536]{0,1:T(8,128)(2,1)} async-done(((bf16[3072,1536]{0,1:T(8,128)(2,1)}), bf16[12288,1536]{0,1:T(8,128)(2,1)}) %all-gather.5.cloned.1.call-update) | async-done | bytes 37748752 | tf_op jit(solution)/shard_map/all_gather | solution.py:44
  256.6 48.9 %copy.36 = bf16[12288,1536]{1,0:T(8,128)(2,1)} copy(bf16[12288,1536]{0,1:T(8,128)(2,1)} %all-gather.5.cloned.1.call-done) | data formatting | bytes 75497472 | tf_op jit(solution)/shard_map/all_gather | solution.py:44
  305.6 33.3 %gather_fusion = bf16[120,128,1536]{2,1,0:T(8,128)(2,1)} fusion(bf16[96,128,1536]{2,1,0:T(8,128)(2,1)} %bitcast.87, s32[1024]{0:T(1024)S(1)} %pad_clamp_fusion.1), kind=kCustom, calls=%fused_computation.clone | custom fusion | bytes 94372320 | tf_op jit(solution)/shard_map/jit(_take)/gather | solution.py:13
  338.8 26.4 %fusion.8 = f32[24,1536,128,1]{1,2,3,0:T(8,128)} fusion(bf16[24,5,128,128]{3,2,1,0:T(8,128)(2,1)} %param.12, bf16[24,5,128,1536]{3,2,1,0:T(8,128)(2,1)} %bitcast.93, pred[24,5]{1,0:T(8,128)(4,1)S(1)} %copy.33), kind=kOutput, calls=%fused_computation.12 | convolution fusion | flops 6063390720 | bytes 69992568 | tf_op jit(solution)/shard_map/jsoi,jsin->jon/dot_general | solution.py:14
  365.2 18.7 copy.38
  383.9 11.5 multiply_convert_fusion.3
  395.4 5.4 all-to-all-start
  400.8 292.1 %all-gather = s32[8,12,5]{1,2,0:T(8,128)S(1)} all-gather(s32[1,12,5]{1,2,0:T(8,128)S(1)} %bitcast.99), channel_id=1, replica_groups=mesh['row'=8,'col'=4] {'row'}, dimensions={0}, use_global_device_ids=true | all-gather | bytes 2160 | tf_op jit(solution)/shard_map/all_gather | solution.py:36
  692.9 0.1 reshape.153
  693.0 0.1 copy.32
  693.2 0.1 copy.39
  693.3 0.2 reshape.158
  693.5 0.0 all-gather.7.cloned.1.call-done
  693.5 6.6 convert_reduce_fusion
  700.2 12.6 copy.40
  712.8 23.6 %gather_fusion.1 = bf16[480,384,128]{2,1,0:T(8,128)(2,1)} fusion(bf16[384,96,128]{2,0,1:T(8,128)(2,1)} %copy.40, s32[1024]{0:T(1024)S(1)} %pad_clamp_fusion), kind=kCustom, calls=%fused_computation.1.clone | custom fusion | bytes 94373760 | tf_op jit(solution)/shard_map/jit(_take)/gather | solution.py:22
  736.4 31.3 %convert_reduce_fusion.2 = (f32[]{:T(128)}, f32[96,384,128,1]{1,2,3,0:T(8,128)}) fusion(f32[96,128]{1,0:T(8,128)S(1)} %broadcast_divide_fusion, bf16[96,5,128,128]{3,2,1,0:T(8,128)(2,1)} %all-gather.7.cloned.1.call-done, bf16[96,5,384,128]{3,2,1,0:T(8,128)(2,1)} %bitcast.89, pred[96,5]{1,0:T(8,128)(4,1)S(1)} %copy.32), kind=kOutput, calls=%fused_computation.37 | convolution fusion | flops 6082265088 | bytes 81838560 | tf_op jit(solution)/shard_map/cisk,isok->cio/dot_general | solution.py:23
  767.7 11.8 multiply_convert_fusion.2
  779.5 5.1 all-to-all-start.1
  784.6 0.0 all-gather.9.cloned.1.call-start
  784.6 220.6 %all-reduce = (f32[]{:T(128)}, f32[]{:T(128)}) all-reduce(f32[]{:T(128)} %get-tuple-element.11, f32[]{:T(128)} %get-tuple-element.9), channel_id=1, replica_groups=mesh['row'=8,'col'=4] {'row','col'}, use_global_device_ids=true, to_apply=%region_3.6 | all-reduce | flops 2 | bytes 16 | tf_op jit(solution)/shard_map/psum | solution.py:50
  1006.5 12.4 multiply_bitcast_fusion.1
  1018.9 7.6 copy.52
  1026.5 12.7 fusion.21
  1039.2 227.3 %all-gather.9.cloned.1.call-done = bf16[12288,1536]{0,1:T(8,128)(2,1)} async-done(((bf16[3072,1536]{0,1:T(8,128)(2,1)}), bf16[12288,1536]{0,1:T(8,128)(2,1)}) %all-gather.9.cloned.1.call-update) | async-done | bytes 37748752 | tf_op jit(solution)/shard_map/all_gather | solution.py:44
  1266.6 48.7 %copy.42 = bf16[12288,1536]{1,0:T(8,128)(2,1)} copy(bf16[12288,1536]{0,1:T(8,128)(2,1)} %all-gather.9.cloned.1.call-done) | data formatting | bytes 75497472 | tf_op jit(solution)/shard_map/all_gather | solution.py:44
  1315.2 33.3 %gather_fusion.2 = bf16[120,128,1536]{2,1,0:T(8,128)(2,1)} fusion(bf16[96,128,1536]{2,1,0:T(8,128)(2,1)} %bitcast.86, s32[1024]{0:T(1024)S(1)} %copy-done.5), kind=kCustom, calls=%fused_computation.2.clone | custom fusion | bytes 94372320 | tf_op jit(solution)/shard_map/jit(_take)/gather | solution.py:13
  1348.5 24.3 %fusion.5 = f32[24,1536,128,1]{1,2,3,0:T(8,128)} fusion(bf16[24,5,128,128]{3,2,1,0:T(8,128)(2,1)} %param.12, bf16[24,5,128,1536]{3,2,1,0:T(8,128)(2,1)} %bitcast.92, pred[24,5]{1,0:T(8,128)(4,1)S(1)} %copy-done.15), kind=kOutput, calls=%fused_computation.9 | convolution fusion | flops 6063390720 | bytes 69992568 | tf_op jit(solution)/shard_map/jsoi,jsin->jon/dot_general | solution.py:14
  1372.8 18.7 copy.44
  1391.5 7.6 multiply_convert_fusion.1
  1399.1 212.8 %all_to_all.46 = bf16[8,384,1536]{1,2,0:T(8,128)(2,1)} all-to-all(bf16[8,384,1536]{1,2,0:T(8,128)(2,1)S(1)} %multiply_convert_fusion.1), channel_id=1, replica_groups=mesh['row'=8,'col'=4] {'row'}, dimensions={0} | all-to-all | bytes 18874368 | tf_op jit(solution)/shard_map/all_to_all | solution.py:46
  1611.9 12.6 copy.46
  1624.5 23.7 %gather_fusion.3 = bf16[480,384,128]{2,1,0:T(8,128)(2,1)} fusion(bf16[384,96,128]{2,0,1:T(8,128)(2,1)} %copy.46, s32[1024]{0:T(1024)S(1)} %copy-done.1), kind=kCustom, calls=%fused_computation.3.clone | custom fusion | bytes 94373760 | tf_op jit(solution)/shard_map/jit(_take)/gather | solution.py:22
  1648.2 31.3 %convert_reduce_fusion.1 = (f32[]{:T(128)}, f32[96,384,128,1]{1,2,3,0:T(8,128)}) fusion(f32[96,128]{1,0:T(8,128)S(1)} %copy-done.7, bf16[96,5,128,128]{3,2,1,0:T(8,128)(2,1)} %all-gather.7.cloned.1.call-done, bf16[96,5,384,128]{3,2,1,0:T(8,128)(2,1)} %bitcast.88, pred[96,5]{1,0:T(8,128)(4,1)S(1)} %copy-done.12), kind=kOutput, calls=%fused_computation.33 | convolution fusion | flops 6082265088 | bytes 81838560 | tf_op jit(solution)/shard_map/cisk,isok->cio/dot_general | solution.py:23
  1679.5 11.8 multiply_convert_fusion
  1691.3 5.1 all-to-all-start.3
  1696.4 226.1 %psum.23 = f32[]{:T(128)} all-reduce(f32[]{:T(128)} %get-tuple-element.13), channel_id=1, replica_groups=mesh['row'=8,'col'=4] {'row','col'}, use_global_device_ids=true, to_apply=%region_7.10 | all-reduce | flops 1 | bytes 8 | tf_op jit(solution)/shard_map/psum | solution.py:50
  1923.2 12.4 multiply_bitcast_fusion
  1935.5 7.6 copy.53
  1943.1 15.5 fusion.23
  (48 shorter events, 0.2 us)
Async XLA Ops:
  6.5 20.8 %copy-start.10 = (s32[24,5]{0,1:T(8,128)S(1)}, s32[24,5]{0,1:T(8,128)}, u32[]{:S(2)}) copy-start(s32[24,5]{0,1:T(8,128)} %param.13) | copy-start | bytes 1444
  6.5 250.1 %all-gather.5.cloned.1.call-start = ((), (), s32[]{:S(2)}) async-start(), calls=%async_computation.4 | async-start | bytes 47185920 | tf_op jit(solution)/shard_map/all_gather | solution.py:44
  26.6 666.9 %all-gather.7.cloned.1.call-start = ((), (), s32[]{:S(2)}) async-start(), calls=%async_computation.5 | async-start | bytes 17694720 | tf_op jit(solution)/shard_map/all_gather | solution.py:35
  27.4 311.4 %copy-start.14 = (pred[24,5]{1,0:T(8,128)(4,1)}, pred[24,5]{1,0:T(8,128)(4,1)S(1)}, u32[]{:S(2)}) copy-start(pred[24,5]{1,0:T(8,128)(4,1)S(1)} %copy.33) | copy-start | bytes 364
  30.4 353.5 %copy-start.8 = (f32[8,384]{1,0:T(8,128)}, f32[8,384]{1,0:T(8,128)S(1)}, u32[]{:S(2)}) copy-start(f32[8,384]{1,0:T(8,128)S(1)} %div.47) | copy-start | bytes 36868
  30.4 275.1 %copy-start.4 = (s32[1024]{0:T(1024)}, s32[1024]{0:T(1024)S(1)}, u32[]{:S(2)}) copy-start(s32[1024]{0:T(1024)S(1)} %pad_clamp_fusion.1) | copy-start | bytes 12292
  383.9 16.9 copy-start.13
  395.4 304.7 %all-to-all-start = ((bf16[8,384,1536]{1,2,0:T(8,128)(2,1)}), bf16[8,384,1536]{1,2,0:T(8,128)(2,1)}, u32[]{:S(2)}, u32[]{:S(2)}) async-start(bf16[8,384,1536]{1,2,0:T(8,128)(2,1)} %multiply_convert_fusion.3), calls=%async_computation | async-start | bytes 18874368 | tf_op jit(solution)/shard_map/all_to_all | solution.py:46
  693.1 43.3 %copy-start.11 = (pred[96,5]{1,0:T(8,128)(4,1)}, pred[96,5]{1,0:T(8,128)(4,1)S(1)}, u32[]{:S(2)}) copy-start(pred[96,5]{1,0:T(8,128)(4,1)S(1)} %copy.32) | copy-start | bytes 1444
  693.4 43.0 %copy-start = (s32[1024]{0:T(1024)}, s32[1024]{0:T(1024)S(1)}, u32[]{:S(2)}) copy-start(s32[1024]{0:T(1024)S(1)} %pad_clamp_fusion) | copy-start | bytes 12292
  700.1 36.3 %copy-start.6 = (f32[96,128]{1,0:T(8,128)}, f32[96,128]{1,0:T(8,128)S(1)}, u32[]{:S(2)}) copy-start(f32[96,128]{1,0:T(8,128)S(1)} %broadcast_divide_fusion) | copy-start | bytes 147460
  700.1 67.6 %copy-start.2 = (f32[8,1536]{1,0:T(8,128)}, f32[8,1536]{1,0:T(8,128)S(1)}, u32[]{:S(2)}) copy-start(f32[8,1536]{1,0:T(8,128)S(1)} %div.50) | copy-start | bytes 147460
  779.5 227.0 %all-to-all-start.1 = ((bf16[384,8,1536]{0,2,1:T(8,128)(2,1)}), bf16[384,8,1536]{0,2,1:T(8,128)(2,1)}, u32[]{:S(2)}, u32[]{:S(2)}) async-start(bf16[384,8,1536]{0,2,1:T(8,128)(2,1)} %multiply_convert_fusion.2), calls=%async_computation.1 | async-start | bytes 18874368 | tf_op jit(solution)/shard_map/all_to_all | solution.py:49
  784.6 482.0 %all-gather.9.cloned.1.call-start = ((), (), s32[]{:S(2)}) async-start(), calls=%async_computation.6 | async-start | bytes 47185920 | tf_op jit(solution)/shard_map/all_gather | solution.py:44
  1039.2 276.0 %copy-start.5 = (s32[1024]{0:T(1024)S(1)}, s32[1024]{0:T(1024)}, u32[]{:S(2)}) copy-start(s32[1024]{0:T(1024)} %copy-done.4) | copy-start | bytes 12292
  1315.2 33.3 %copy-start.15 = (pred[24,5]{1,0:T(8,128)(4,1)S(1)}, pred[24,5]{1,0:T(8,128)(4,1)}, u32[]{:S(2)}) copy-start(pred[24,5]{1,0:T(8,128)(4,1)} %copy-done.14) | copy-start | bytes 364
  1372.8 18.7 copy-start.9
  1399.1 225.5 %copy-start.1 = (s32[1024]{0:T(1024)S(1)}, s32[1024]{0:T(1024)}, u32[]{:S(2)}) copy-start(s32[1024]{0:T(1024)} %copy-done) | copy-start | bytes 12292
  1624.5 23.7 %copy-start.7 = (f32[96,128]{1,0:T(8,128)S(1)}, f32[96,128]{1,0:T(8,128)}, u32[]{:S(2)}) copy-start(f32[96,128]{1,0:T(8,128)} %copy-done.6) | copy-start | bytes 147460
  1624.5 23.7 %copy-start.12 = (pred[96,5]{1,0:T(8,128)(4,1)S(1)}, pred[96,5]{1,0:T(8,128)(4,1)}, u32[]{:S(2)}) copy-start(pred[96,5]{1,0:T(8,128)(4,1)} %copy-done.11) | copy-start | bytes 1444
  1648.2 31.3 %copy-start.3 = (f32[8,1536]{1,0:T(8,128)S(1)}, f32[8,1536]{1,0:T(8,128)}, u32[]{:S(2)}) copy-start(f32[8,1536]{1,0:T(8,128)} %copy-done.2) | copy-start | bytes 147460
  1691.3 231.9 %all-to-all-start.3 = ((bf16[384,8,1536]{0,2,1:T(8,128)(2,1)}), bf16[384,8,1536]{0,2,1:T(8,128)(2,1)}, u32[]{:S(2)}, u32[]{:S(2)}) async-start(bf16[384,8,1536]{0,2,1:T(8,128)(2,1)} %multiply_convert_fusion), calls=%async_computation.3 | async-start | bytes 18874368 | tf_op jit(solution)/shard_map/all_to_all | solution.py:49
Sparse Core Ops, SparseCore 0:
  26.7 229.8 all-gather.4
  258.8 288.7 all-gather.6
  1039.4 227.1 all-gather.8
where the time goes:
time: 1970 us
  blocking collectives  952 us (48%)
  waiting for transfers between devices  454 us (23%)
  local copies, waits for them, and re-layouts  290 us (15%)
  other arithmetic  125 us (6%)
  matrix products  113 us (6%)
    all_gather x2, waiting for transfers between devices, local(): gathered = lax.all_gather(current, 'col', axis=0, tiled=True)  454 us
    psum x2, blocking collectives, local(): slab_sum = lax.psum(partial_value, ('row', 'col'))  447 us
    all_gather x1, blocking collectives, local(): lax.all_gather(columns_first, 'row', axis=0, tiled=True)  292 us
    all_to_all x1, blocking collectives, local(): lax.all_to_all(mixed_cols, 'row', split_axis=0, concat_axis=1, tiled=True)  213 us
    all_gather x2, local copies, waits for them, and re-layouts, local(): gathered = lax.all_gather(current, 'col', axis=0, tiled=True)  97.6 us
    gather x2, local copies, waits for them, and re-layouts, second_product(): picked = jnp.take(blocks, columns, axis=0)  66.5 us
    dot_general x2, matrix products, first_product(): jnp.einsum('cisk,isok->cio', picked, tile_set, preferred_element_type=jnp...  62.6 us
    dot_general x2, matrix products, second_product(): jnp.einsum('jsoi,jsin->jon', tile_set, picked, preferred_element_type=jnp...  50.7 us
  transfers between devices with their start and end apart: 6, of which 2 were waited for; matrix products, arithmetic and copies ran while one was open for 8% of the time, Pallas kernels for 0%

commit v1 on v0

--- a/solution.py
+++ b/solution.py
@@ -1,10 +1,28 @@
+import functools
 import jax
 import jax.numpy as jnp
 from jax import lax
 from jax.sharding import PartitionSpec as P
+from jax.lax import all_to_all, axis_size
 
 ITERS = 2
 mixing = 0.8
+
+
+def wrap_column_all(slab_in, link_axis):
+    mat_out = jnp.concatenate(
+        all_to_all(
+            jnp.stack([slab_in for _ in range(axis_size(link_axis))]),
+            concat_axis=0,
+            axis_name=link_axis,
+            split_axis=0,
+        ),
+        axis=0,
+    )
+    return mat_out
+
+
+step_on_threads_in = functools.partial(wrap_column_all, link_axis="row")
 
 
 def second_product(features, tile_set, columns, inverse):
@@ -33,7 +51,7 @@
     )
     all_first, all_columns = (
         lax.all_gather(tiles_first, "row", axis=0, tiled=True),
-        lax.all_gather(columns_first, "row", axis=0, tiled=True),
+        step_on_threads_in(columns_first),
     )
     inverse_first = 1.0 / jnp.sum(all_first, axis=(1, 3), dtype=jnp.float32).reshape(-1)
     inverse_second = 1.0 / jnp.sum(tiles_second, axis=(1, 3), dtype=jnp.float32).reshape(-1)

time: 1970 us -> 1950 us (0.990)
  blocking collectives: 952 us -> 664 us
  waiting for transfers between devices: 454 us -> 710 us
    all_gather x1 -> x0, blocking collectives: 292 us -> none  [local(): lax.all_gather(columns_first, 'row', axis=0, tiled=True)]
    all_gather x1, waiting for transfers between devices: 0.02 us -> 146 us  [local(): lax.all_gather(tiles_first, 'row', axis=0, tiled=True)]
    all_to_all x1, waiting for transfers between devices: 0.01 us -> 119 us  [local(): lax.all_to_all(mixed_cols, 'row', split_axis=0, concat_axis=1, tiled=True)]
  transfers between devices with their start and end apart: 6 -> 7, of which waited for: 2 -> 4; matrix products, arithmetic and copies ran while one was open for 8% -> 8% of each run, Pallas kernels for 0% -> 0%
where the time goes in v1:
time: 1950 us; the launch traced here: 1940 us
  waiting for transfers between devices  710 us (36%)
  blocking collectives  664 us (34%)
  local copies, waits for them, and re-layouts  291 us (15%)
  other arithmetic  126 us (6%)
  matrix products  113 us (6%)
  starting transfers between devices  22.8 us (1%)
    psum x2, blocking collectives, local(): slab_sum = lax.psum(partial_value, ('row', 'col'))  453 us
    all_gather x2, waiting for transfers between devices, local(): gathered = lax.all_gather(current, 'col', axis=0, tiled=True)  445 us
    all_to_all x1, blocking collectives, local(): lax.all_to_all(mixed_cols, 'row', split_axis=0, concat_axis=1, tiled=True)  212 us
    all_gather x1, waiting for transfers between devices, local(): lax.all_gather(tiles_first, 'row', axis=0, tiled=True)  146 us
    all_to_all x1, waiting for transfers between devices, local(): lax.all_to_all(mixed_cols, 'row', split_axis=0, concat_axis=1, tiled=True)  119 us
    all_gather x2, local copies, waits for them, and re-layouts, local(): gathered = lax.all_gather(current, 'col', axis=0, tiled=True)  97.6 us
    gather x2, local copies, waits for them, and re-layouts, second_product(): picked = jnp.take(blocks, columns, axis=0)  66.4 us
    dot_general x2, matrix products, first_product(): jnp.einsum('cisk,isok->cio', picked, tile_set, preferred_element_type=jnp...  62.4 us
  transfers between devices with their start and end apart: 7, of which 4 were waited for; matrix products, arithmetic and copies ran while one was open for 8% of the time, Pallas kernels for 0%

profile of v1, /device:TPU:0, one launch (start us, length us, event | category | flops | bytes accessed | tf_op | source)
XLA Modules:
  0.0 1942.4 jit_solution(1566009299612423928)
XLA Ops:
  6.5 20.1 %fusion.28 = (f32[]{:T(128)}, bf16[3072,1536]{0,1:T(8,128)(2,1)}) fusion(f32[1536,3072]{1,0:T(8,128)} %param.9), kind=kLoop, calls=%fused_computation.55 | loop fusion | flops 9437183 | bytes 28311556 | tf_op jit(solution)/shard_map/reduce_sum | solution.py:58
  26.7 0.7 all-gather.6.cloned.1.call-update
  27.4 0.6 stack.2
  28.1 7.3 all-to-all-start.1
  35.4 0.1 copy.33
  35.5 0.1 copy.37
  35.6 0.1 reshape.158
  35.7 3.7 convert_reduce_fusion.3
  39.4 217.3 %all-gather.4.cloned.1.call-done = bf16[12288,1536]{0,1:T(8,128)(2,1)} async-done(((bf16[3072,1536]{0,1:T(8,128)(2,1)}), bf16[12288,1536]{0,1:T(8,128)(2,1)}) %all-gather.4.cloned.1.call-update) | async-done | bytes 37748752 | tf_op jit(solution)/shard_map/all_gather | solution.py:62
  256.7 49.0 %copy.36 = bf16[12288,1536]{1,0:T(8,128)(2,1)} copy(bf16[12288,1536]{0,1:T(8,128)(2,1)} %all-gather.4.cloned.1.call-done) | data formatting | bytes 75497472 | tf_op jit(solution)/shard_map/all_gather | solution.py:62
  305.7 33.2 %gather_fusion = bf16[120,128,1536]{2,1,0:T(8,128)(2,1)} fusion(bf16[96,128,1536]{2,1,0:T(8,128)(2,1)} %bitcast.86, s32[1024]{0:T(1024)S(1)} %pad_clamp_fusion.1), kind=kCustom, calls=%fused_computation.clone | custom fusion | bytes 94372320 | tf_op jit(solution)/shard_map/jit(_take)/gather | solution.py:31
  338.9 26.4 %fusion.8 = f32[24,1536,128,1]{1,2,3,0:T(8,128)} fusion(bf16[24,5,128,128]{3,2,1,0:T(8,128)(2,1)} %param.12, bf16[24,5,128,1536]{3,2,1,0:T(8,128)(2,1)} %bitcast.92, pred[24,5]{1,0:T(8,128)(4,1)S(1)} %copy.33), kind=kOutput, calls=%fused_computation.12 | convolution fusion | flops 6063390720 | bytes 69992568 | tf_op jit(solution)/shard_map/jsoi,jsin->jon/dot_general | solution.py:32
  365.2 18.7 copy.38
  383.9 11.5 multiply_convert_fusion.3
  395.4 5.3 all-to-all-start
  400.7 0.1 reshape.112
  400.8 0.1 copy.32
  401.0 0.1 copy.39
  401.1 0.2 reshape.162
  401.3 146.4 %all-gather.6.cloned.1.call-done = bf16[96,5,128,128]{3,2,1,0:T(8,128)(2,1)} async-done(((bf16[12,5,128,128]{3,2,1,0:T(8,128)(2,1)}), bf16[96,5,128,128]{3,2,1,0:T(8,128)(2,1)}) %all-gather.6.cloned.1.call-update) | async-done | bytes 15728656 | tf_op jit(solution)/shard_map/all_gather | solution.py:53
  547.7 6.6 convert_reduce_fusion
  554.3 118.6 %all-to-all-done = bf16[8,384,1536]{1,2,0:T(8,128)(2,1)} async-done(((bf16[8,384,1536]{1,2,0:T(8,128)(2,1)}), bf16[8,384,1536]{1,2,0:T(8,128)(2,1)}, u32[]{:S(2)}, u32[]{:S(2)}) %all-to-all-start) | async-done | bytes 9437216 | tf_op jit(solution)/shard_map/all_to_all | solution.py:64
  672.9 12.6 copy.40
  685.5 23.7 %gather_fusion.1 = bf16[480,384,128]{2,1,0:T(8,128)(2,1)} fusion(bf16[384,96,128]{2,0,1:T(8,128)(2,1)} %copy.40, s32[1024]{0:T(1024)S(1)} %pad_clamp_fusion), kind=kCustom, calls=%fused_computation.1.clone | custom fusion | bytes 94373760 | tf_op jit(solution)/shard_map/jit(_take)/gather | solution.py:40
  709.2 31.2 %convert_reduce_fusion.2 = (f32[]{:T(128)}, f32[96,384,128,1]{1,2,3,0:T(8,128)}) fusion(f32[96,128]{1,0:T(8,128)S(1)} %broadcast_divide_fusion, bf16[96,5,128,128]{3,2,1,0:T(8,128)(2,1)} %all-gather.6.cloned.1.call-done, bf16[96,5,384,128]{3,2,1,0:T(8,128)(2,1)} %bitcast.88, pred[96,5]{1,0:T(8,128)(4,1)S(1)} %copy.32), kind=kOutput, calls=%fused_computation.37 | convolution fusion | flops 6082265088 | bytes 81838560 | tf_op jit(solution)/shard_map/cisk,isok->cio/dot_general | solution.py:41
  740.4 11.8 multiply_convert_fusion.2
  752.2 5.1 all-to-all-start.2
  757.2 0.0 all-gather.8.cloned.1.call-start
  757.3 226.2 %all-reduce = (f32[]{:T(128)}, f32[]{:T(128)}) all-reduce(f32[]{:T(128)} %get-tuple-element.11, f32[]{:T(128)} %get-tuple-element.9), channel_id=1, replica_groups=mesh['row'=8,'col'=4] {'row','col'}, use_global_device_ids=true, to_apply=%region_3.6 | all-reduce | flops 2 | bytes 16 | tf_op jit(solution)/shard_map/psum | solution.py:68
  984.7 12.4 multiply_bitcast_fusion.1
  997.1 7.6 copy.52
  1004.7 12.7 fusion.21
  1017.4 227.3 %all-gather.8.cloned.1.call-done = bf16[12288,1536]{0,1:T(8,128)(2,1)} async-done(((bf16[3072,1536]{0,1:T(8,128)(2,1)}), bf16[12288,1536]{0,1:T(8,128)(2,1)}) %all-gather.8.cloned.1.call-update) | async-done | bytes 37748752 | tf_op jit(solution)/shard_map/all_gather | solution.py:62
  1244.7 48.7 %copy.42 = bf16[12288,1536]{1,0:T(8,128)(2,1)} copy(bf16[12288,1536]{0,1:T(8,128)(2,1)} %all-gather.8.cloned.1.call-done) | data formatting | bytes 75497472 | tf_op jit(solution)/shard_map/all_gather | solution.py:62
  1293.4 33.2 %gather_fusion.2 = bf16[120,128,1536]{2,1,0:T(8,128)(2,1)} fusion(bf16[96,128,1536]{2,1,0:T(8,128)(2,1)} %bitcast.85, s32[1024]{0:T(1024)S(1)} %copy-done.5), kind=kCustom, calls=%fused_computation.2.clone | custom fusion | bytes 94372320 | tf_op jit(solution)/shard_map/jit(_take)/gather | solution.py:31
  1326.5 24.4 %fusion.5 = f32[24,1536,128,1]{1,2,3,0:T(8,128)} fusion(bf16[24,5,128,128]{3,2,1,0:T(8,128)(2,1)} %param.12, bf16[24,5,128,1536]{3,2,1,0:T(8,128)(2,1)} %bitcast.91, pred[24,5]{1,0:T(8,128)(4,1)S(1)} %copy-done.15), kind=kOutput, calls=%fused_computation.9 | convolution fusion | flops 6063390720 | bytes 69992568 | tf_op jit(solution)/shard_map/jsoi,jsin->jon/dot_general | solution.py:32
  1350.9 18.6 copy.44
  1369.6 7.6 multiply_convert_fusion.1
  1377.2 211.8 %all_to_all.51 = bf16[8,384,1536]{1,2,0:T(8,128)(2,1)} all-to-all(bf16[8,384,1536]{1,2,0:T(8,128)(2,1)S(1)} %multiply_convert_fusion.1), channel_id=1, replica_groups=mesh['row'=8,'col'=4] {'row'}, dimensions={0} | all-to-all | bytes 18874368 | tf_op jit(solution)/shard_map/all_to_all | solution.py:64
  1589.0 12.6 copy.46
  1601.6 23.7 %gather_fusion.3 = bf16[480,384,128]{2,1,0:T(8,128)(2,1)} fusion(bf16[384,96,128]{2,0,1:T(8,128)(2,1)} %copy.46, s32[1024]{0:T(1024)S(1)} %copy-done.1), kind=kCustom, calls=%fused_computation.3.clone | custom fusion | bytes 94373760 | tf_op jit(solution)/shard_map/jit(_take)/gather | solution.py:40
  1625.3 31.2 %convert_reduce_fusion.1 = (f32[]{:T(128)}, f32[96,384,128,1]{1,2,3,0:T(8,128)}) fusion(f32[96,128]{1,0:T(8,128)S(1)} %copy-done.7, bf16[96,5,128,128]{3,2,1,0:T(8,128)(2,1)} %all-gather.6.cloned.1.call-done, bf16[96,5,384,128]{3,2,1,0:T(8,128)(2,1)} %bitcast.87, pred[96,5]{1,0:T(8,128)(4,1)S(1)} %copy-done.12), kind=kOutput, calls=%fused_computation.33 | convolution fusion | flops 6082265088 | bytes 81838560 | tf_op jit(solution)/shard_map/cisk,isok->cio/dot_general | solution.py:41
  1656.5 11.8 multiply_convert_fusion
  1668.3 5.1 all-to-all-start.4
  1673.4 226.3 %psum.23 = f32[]{:T(128)} all-reduce(f32[]{:T(128)} %get-tuple-element.13), channel_id=1, replica_groups=mesh['row'=8,'col'=4] {'row','col'}, use_global_device_ids=true, to_apply=%region_7.10 | all-reduce | flops 1 | bytes 8 | tf_op jit(solution)/shard_map/psum | solution.py:68
  1900.4 12.4 multiply_bitcast_fusion
  1912.7 7.6 copy.53
  1920.3 15.5 fusion.23
  (50 shorter events, 0.2 us)
Async XLA Ops:
  6.5 20.9 %copy-start.13 = (s32[12,5]{0,1:T(8,128)S(1)}, s32[12,5]{0,1:T(8,128)}, u32[]{:S(2)}) copy-start(s32[12,5]{0,1:T(8,128)} %param.11) | copy-start | bytes 724
  6.5 28.8 %copy-start.10 = (s32[24,5]{0,1:T(8,128)S(1)}, s32[24,5]{0,1:T(8,128)}, u32[]{:S(2)}) copy-start(s32[24,5]{0,1:T(8,128)} %param.13) | copy-start | bytes 1444
  6.5 250.2 %all-gather.4.cloned.1.call-start = ((), (), s32[]{:S(2)}) async-start(), calls=%async_computation.5 | async-start | bytes 47185920 | tf_op jit(solution)/shard_map/all_gather | solution.py:62
  26.7 521.0 %all-gather.6.cloned.1.call-start = ((), (), s32[]{:S(2)}) async-start(), calls=%async_computation.6 | async-start | bytes 17694720 | tf_op jit(solution)/shard_map/all_gather | solution.py:53
  28.1 367.4 %all-to-all-start.1 = ((s32[8,12,5]{1,2,0:T(8,128)}), s32[8,12,5]{1,2,0:T(8,128)S(1)}, u32[]{:S(2)}, u32[]{:S(2)}) async-start(s32[8,12,5]{1,2,0:T(8,128)} %stack.2), calls=%async_computation.1 | async-start | bytes 65536 | tf_op jit(solution)/shard_map/all_to_all | solution.py:14
  35.5 303.4 %copy-start.14 = (pred[24,5]{1,0:T(8,128)(4,1)}, pred[24,5]{1,0:T(8,128)(4,1)S(1)}, u32[]{:S(2)}) copy-start(pred[24,5]{1,0:T(8,128)(4,1)S(1)} %copy.33) | copy-start | bytes 364
  39.4 344.5 %copy-start.8 = (f32[8,384]{1,0:T(8,128)}, f32[8,384]{1,0:T(8,128)S(1)}, u32[]{:S(2)}) copy-start(f32[8,384]{1,0:T(8,128)S(1)} %div.47) | copy-start | bytes 36868
  39.4 266.3 %copy-start.4 = (s32[1024]{0:T(1024)}, s32[1024]{0:T(1024)S(1)}, u32[]{:S(2)}) copy-start(s32[1024]{0:T(1024)S(1)} %pad_clamp_fusion.1) | copy-start | bytes 12292
  395.4 277.5 %all-to-all-start = ((bf16[8,384,1536]{1,2,0:T(8,128)(2,1)}), bf16[8,384,1536]{1,2,0:T(8,128)(2,1)}, u32[]{:S(2)}, u32[]{:S(2)}) async-start(bf16[8,384,1536]{1,2,0:T(8,128)(2,1)} %multiply_convert_fusion.3), calls=%async_computation | async-start | bytes 18874368 | tf_op jit(solution)/shard_map/all_to_all | solution.py:64
  400.9 308.2 %copy-start.11 = (pred[96,5]{1,0:T(8,128)(4,1)}, pred[96,5]{1,0:T(8,128)(4,1)S(1)}, u32[]{:S(2)}) copy-start(pred[96,5]{1,0:T(8,128)(4,1)S(1)} %copy.32) | copy-start | bytes 1444
  401.2 307.9 %copy-start = (s32[1024]{0:T(1024)}, s32[1024]{0:T(1024)S(1)}, u32[]{:S(2)}) copy-start(s32[1024]{0:T(1024)S(1)} %pad_clamp_fusion) | copy-start | bytes 12292
  554.3 154.9 %copy-start.6 = (f32[96,128]{1,0:T(8,128)}, f32[96,128]{1,0:T(8,128)S(1)}, u32[]{:S(2)}) copy-start(f32[96,128]{1,0:T(8,128)S(1)} %broadcast_divide_fusion) | copy-start | bytes 147460
  554.3 186.1 %copy-start.2 = (f32[8,1536]{1,0:T(8,128)}, f32[8,1536]{1,0:T(8,128)S(1)}, u32[]{:S(2)}) copy-start(f32[8,1536]{1,0:T(8,128)S(1)} %div.50) | copy-start | bytes 147460
  752.2 232.6 %all-to-all-start.2 = ((bf16[384,8,1536]{0,2,1:T(8,128)(2,1)}), bf16[384,8,1536]{0,2,1:T(8,128)(2,1)}, u32[]{:S(2)}, u32[]{:S(2)}) async-start(bf16[384,8,1536]{0,2,1:T(8,128)(2,1)} %multiply_convert_fusion.2), calls=%async_computation.2 | async-start | bytes 18874368 | tf_op jit(solution)/shard_map/all_to_all | solution.py:67
  757.2 487.5 %all-gather.8.cloned.1.call-start = ((), (), s32[]{:S(2)}) async-start(), calls=%async_computation.7 | async-start | bytes 47185920 | tf_op jit(solution)/shard_map/all_gather | solution.py:62
  1017.4 275.9 %copy-start.5 = (s32[1024]{0:T(1024)S(1)}, s32[1024]{0:T(1024)}, u32[]{:S(2)}) copy-start(s32[1024]{0:T(1024)} %copy-done.4) | copy-start | bytes 12292
  1293.4 33.2 %copy-start.15 = (pred[24,5]{1,0:T(8,128)(4,1)S(1)}, pred[24,5]{1,0:T(8,128)(4,1)}, u32[]{:S(2)}) copy-start(pred[24,5]{1,0:T(8,128)(4,1)} %copy-done.14) | copy-start | bytes 364
  1350.9 18.6 copy-start.9
  1377.2 224.4 %copy-start.1 = (s32[1024]{0:T(1024)S(1)}, s32[1024]{0:T(1024)}, u32[]{:S(2)}) copy-start(s32[1024]{0:T(1024)} %copy-done) | copy-start | bytes 12292
  1601.6 23.7 %copy-start.7 = (f32[96,128]{1,0:T(8,128)S(1)}, f32[96,128]{1,0:T(8,128)}, u32[]{:S(2)}) copy-start(f32[96,128]{1,0:T(8,128)} %copy-done.6) | copy-start | bytes 147460
  1601.6 23.7 %copy-start.12 = (pred[96,5]{1,0:T(8,128)(4,1)S(1)}, pred[96,5]{1,0:T(8,128)(4,1)}, u32[]{:S(2)}) copy-start(pred[96,5]{1,0:T(8,128)(4,1)} %copy-done.11) | copy-start | bytes 1444
  1625.3 31.2 %copy-start.3 = (f32[8,1536]{1,0:T(8,128)S(1)}, f32[8,1536]{1,0:T(8,128)}, u32[]{:S(2)}) copy-start(f32[8,1536]{1,0:T(8,128)} %copy-done.2) | copy-start | bytes 147460
  1668.3 232.0 %all-to-all-start.4 = ((bf16[384,8,1536]{0,2,1:T(8,128)(2,1)}), bf16[384,8,1536]{0,2,1:T(8,128)(2,1)}, u32[]{:S(2)}, u32[]{:S(2)}) async-start(bf16[384,8,1536]{0,2,1:T(8,128)(2,1)} %multiply_convert_fusion), calls=%async_computation.4 | async-start | bytes 18874368 | tf_op jit(solution)/shard_map/all_to_all | solution.py:67
Sparse Core Ops, SparseCore 0:
  26.8 229.8 all-gather.3
  258.9 288.7 all-gather.5
  1017.5 227.1 all-gather.7
